TPU v7x, 32 devices: a whole 2x2x4 slice. The times are simulated.
32 devices in a mesh: seq: 8 (over z, x), chan: 4 (over y, core).
Axes of the slice: x: 2, y: 2, z: 4, core: 2. Of those that a mesh axis runs over, the one named last changes fastest.
Arguments:
- x_in: bfloat16 [6144, 5120], P('seq', 'chan'), may hold values from -120 to 120
- z_gate: bfloat16 [6144, 5120], P('seq', 'chan'), may hold values from -6 to 6
- b_proj: bfloat16 [6144, 128], P('seq'), may hold values from -6 to 6
- c_proj: bfloat16 [6144, 128], P('seq'), may hold values from -6 to 6
- dt_step: float32 [80, 6144], P('chan', 'seq'), may hold values from 0 to 1
- a_log: float32 [80], P('chan'), may hold values from -0.35 to 0.35
- skip_gain: float32 [80], P('chan'), may hold values from 0.5 to 1.5
- norm_gain: float32 [5120], P('chan'), may hold values from 0.5 to 1.5
- out_weight: bfloat16 [2560, 5120], P('seq', 'chan'), may hold values from -0.078125 to 0.078125
- out_grad: bfloat16 [6144, 2560], P('seq'), may hold values from -6 to 6
Outputs:
- d_x: bfloat16 [6144, 5120], P('seq', 'chan')
- d_z: bfloat16 [6144, 5120], P('seq', 'chan')
- d_dt: float32 [80, 6144], P('chan', 'seq')
- d_out_weight: float32 [2560, 5120], P('seq', 'chan')
All inputs are finite; a program needn't handle non-finite values.
Results may differ from a plain program's by a relative error of at most 0.005.
Values may be sent and summed in bfloat16 or wider, within the bound.
A program may use at most 128 MiB of HBM per device.

v0:
```python
from functools import partial

import jax
import jax.numpy as jnp
from jax import lax
from jax.sharding import PartitionSpec as P

GROUP = 256


norm_eps = 1e-05
highest = lax.Precision.HIGHEST


def entering(value, axis, combine, identity, reverse):
    peers, index = (lax.axis_size(axis), lax.axis_index(axis))
    everything = jax.tree.map(lambda part: lax.all_gather(part, axis), value)
    start = jax.tree.map(
        lambda part, zero: jnp.broadcast_to(jnp.asarray(zero, part.dtype), part.shape),
        value,
        identity,
    )

    def turn(k, before):
        at = peers - 1 - k if reverse else k
        reached = at > index if reverse else at < index
        new = combine(before, jax.tree.map(lambda part: part[at], everything))
        return jax.tree.map(lambda a, b: jnp.where(reached, a, b), new, before)

    return lax.fori_loop(0, peers, turn, start)


def group_step(state_in, pieces, decay_rates, skip_gain):
    x_part, dt_part, b_part, c_part = pieces
    log_decay = jnp.cumsum(-decay_rates[:, None] * dt_part, axis=1)
    length = dt_part.shape[1]
    row_ids = lax.broadcasted_iota(jnp.int32, (length, length), 0)
    col_ids = lax.broadcasted_iota(jnp.int32, (length, length), 1)
    causal = (row_ids >= col_ids)[None]
    log_gap = jnp.where(causal, log_decay[:, :, None] - log_decay[:, None, :], 0.0)
    decay_mat = jnp.where(causal, jnp.exp(log_gap), 0.0)
    affinity = jnp.dot(c_part, b_part.T, precision=highest)
    weighted = x_part * jnp.transpose(dt_part)[:, :, None]
    within = jnp.einsum("hts,shp->thp", decay_mat * affinity[None], weighted, precision=highest)
    carried = jnp.transpose(jnp.exp(log_decay))[:, :, None] * jnp.einsum(
        "tn,hpn->thp", c_part, state_in, precision=highest
    )
    output = within + carried + skip_gain[None, :, None] * x_part
    to_end = jnp.exp(log_decay[:, -1:] - log_decay)
    update = jnp.einsum("shp,hs,sn->hpn", weighted, to_end, b_part, precision=highest)
    state_out = jnp.exp(log_decay[:, -1])[:, None, None] * state_in + update
    return (state_out, output)


def ssd_local(x_vals, dt_vals, b_vals, c_vals, decay_rates, skip_gain, state_in):
    length, head_count, head_size = x_vals.shape
    blocks = length // GROUP
    x_blocks = x_vals.reshape(blocks, GROUP, head_count, head_size)
    dt_blocks = jnp.transpose(dt_vals.reshape(head_count, blocks, GROUP), (1, 0, 2))
    b_blocks = b_vals.reshape(blocks, GROUP, -1)
    c_blocks = c_vals.reshape(blocks, GROUP, -1)
    stepper = jax.checkpoint(partial(group_step, decay_rates=decay_rates, skip_gain=skip_gain))
    state_out, outputs = lax.scan(stepper, state_in, (x_blocks, dt_blocks, b_blocks, c_blocks))
    return (outputs.reshape(length, head_count, head_size), state_out)


def combine_pair(earlier, later):
    return (earlier[0] * later[0], later[0][:, None, None] * earlier[1] + later[1])


def shards(
    x_in, z_gate, b_proj, c_proj, dt_step, a_log, skip_gain, norm_gain, out_weight, out_grad
):
    length, width = x_in.shape
    head_count = a_log.shape[0]
    head_size = width // head_count
    decay_rates = jnp.exp(a_log)
    b_vals = b_proj.astype(jnp.float32)
    c_vals = c_proj.astype(jnp.float32)
    zero_state = jnp.zeros((head_count, head_size, b_vals.shape[1]), jnp.float32)
    identity_pair = (jnp.ones((head_count,), jnp.float32), zero_state)

    def local_part(x_arg, dt_arg):
        return ssd_local(x_arg, dt_arg, b_vals, c_vals, decay_rates, skip_gain, zero_state)

    x_vals = x_in.astype(jnp.float32).reshape(length, head_count, head_size)
    (y_local, s_local), pull_local = jax.vjp(local_part, x_vals, dt_step)
    device_decay = jnp.exp(-decay_rates * jnp.sum(dt_step, axis=1))
    scanned = entering((device_decay, s_local), "seq", combine_pair, identity_pair, False)
    state_in = scanned[1]

    def outside_part(dt_arg, state_arg):
        log_run = jnp.cumsum(-decay_rates[:, None] * dt_arg, axis=1)
        return jnp.transpose(jnp.exp(log_run))[:, :, None] * jnp.einsum(
            "tn,hpn->thp", c_vals, state_arg, precision=highest
        )

    y_outside, pull_outside = jax.vjp(outside_part, dt_step, state_in)
    y_vals = (y_local + y_outside).reshape(length, width)
    columns = out_grad
    grad_sum = jnp.dot(
        columns,
        lax.all_gather(out_weight, "seq", axis=0, tiled=True),
        preferred_element_type=jnp.float32,
    )
    grad_norm = grad_sum.astype(jnp.bfloat16)
    z_vals = z_gate.astype(jnp.float32)
    sigmoid_z = jax.nn.sigmoid(z_vals)
    gate_act = z_vals * sigmoid_z
    gated_y = y_vals * gate_act
    full_width = width * lax.axis_size("chan")
    scaled_grad = grad_norm.astype(jnp.float32) * norm_gain
    local_squares = jnp.sum(gated_y * gated_y, axis=1)
    local_dots = jnp.sum(gated_y * scaled_grad, axis=1)
    square_sum = lax.psum(local_squares, "chan")
    dot_sum = lax.psum(local_dots, "chan")
    inverse_scale = lax.rsqrt(square_sum / full_width + norm_eps)
    normed = (gated_y * inverse_scale[:, None] * norm_gain).astype(jnp.bfloat16)
    columns = out_grad
    weight_grad = lax.psum_scatter(
        lax.dot_general(
            columns, normed, (((0,), (0,)), ((), ())), preferred_element_type=jnp.float32
        ),
        "seq",
        scatter_dimension=0,
        tiled=True,
    )
    grad_gated = (
        inverse_scale[:, None] * scaled_grad
        - gated_y * (inverse_scale**3 * dot_sum / full_width)[:, None]
    )
    grad_z = (grad_gated * y_vals * sigmoid_z * (1.0 + z_vals * (1.0 - sigmoid_z))).astype(
        jnp.bfloat16
    )
    grad_y = (grad_gated * gate_act).reshape(length, head_count, head_size)
    grad_dt_outside, grad_local = pull_outside(grad_y)
    scanned_back = entering((device_decay, grad_local), "seq", combine_pair, identity_pair, True)
    grad_out = scanned_back[1]
    grad_x_vals, grad_dt_local = pull_local((grad_y, grad_out))
    grad_decay = jnp.sum(grad_out * state_in, axis=(1, 2))
    grad_dt = grad_dt_local + grad_dt_outside - (grad_decay * device_decay * decay_rates)[:, None]
    grad_x = grad_x_vals.reshape(length, width).astype(jnp.bfloat16)
    return (grad_x, grad_z, grad_dt, weight_grad)


def solution(mesh):
    placed = (
        P("seq", "chan"),
        P("seq", "chan"),
        P("seq", None),
        P("seq", None),
        P("chan", "seq"),
        P("chan"),
        P("chan"),
        P("chan"),
        P("seq", "chan"),
        P("seq", None),
    )
    return jax.shard_map(
        shards,
        mesh=mesh,
        in_specs=placed,
        out_specs=(P("seq", "chan"), P("seq", "chan"), P("chan", "seq"), P("seq", "chan")),
        check_vma=False,
    )
```

profile of v0, /device:TPU:0, one launch (start us, length us, event | category | flops | bytes accessed | tf_op | source)
XLA Modules:
  0.0 705.0 jit_solution(6510634353682534116)
XLA Ops:
  20.1 7.8 %copy.99 = f32[3,256,20,64]{1,3,2,0:T(8,128)} copy(f32[3,256,20,64]{3,2,1,0:T(8,128)} %reshape.342) | data formatting | bytes 7864320
  27.9 142.4 %while.69 = (s32[]{:T(128)}, f32[20,64,128]{2,1,0:T(8,128)S(1)}, f32[3,256,20,64]{1,0,3,2:T(4,128)}, f32[3,20,64,128]{3,2,1,0:T(8,128)}, f32[20,1]{0,1:T(1,128)S...) while((s32[]{:T(128)}, f32[20,64,128]{2,1,0:T(8,128)S(1)}, ...), condition=%wide.region_6.7_spmd.clone.clone, body=%wide.region_3.6_spmd.clone.clone.sunk | while | flops 2122950656 | bytes 33860016 | solution.py:63
  32.1 7.5 %fusion.170 = f32[256,20,64]{0,2,1:T(8,128)S(1)} fusion(f32[256,256]{1,0:T(8,128)S(1)} %fusion.169, f32[20,256]{1,0:T(8,128)S(1)} %bitcast.291, pred[256,256]{1,0:T(8,128)(4,1)S(1)} %get-tuple-element.1208, f32[3,256,20,64]{1,3,2,0:T(8,128)} %get-tuple-element.1204, s32[]{:T(128)S(6)} %copy.177, f32[256,20]{0,1:T(8,128)S(1)} %fusion.167), kind=kOutput, calls=%fused_computation.22.clone.1 | convolution fusion | flops 1012203520 | bytes 3022852 | tf_op jit(solution)/shard_map/jvp()/while/body/eval_jaxpr/hts,shp->thp/dot_general | solution.py:44
  46.4 29.0 %dynamic_update_slice.47 = f32[3,256,20,64]{1,0,3,2:T(4,128)} dynamic-update-slice(f32[3,256,20,64]{1,0,3,2:T(4,128)} %get-tuple-element.1186, f32[1,256,20,64]{1,0,3,2:T(1,128)S(1)} %copy.167, s32[]{:T(128)S(6)} %copy.177, s32[]{:T(128)} %constant.175.clone.1..sunk.2, s32[]{:T(128)} %constant.175.clone.1..sunk.2, s32[]{:T(128)} %constant.175.clone.1..sunk.2) | dynamic-update-slice | bytes 2621444 | tf_op jit(solution)/shard_map/jvp()/while/body/jit(dynamic_update_index_in_dim)/dynamic_update_slice | solution.py:63
  93.9 29.0 %dynamic_update_slice.47 = f32[3,256,20,64]{1,0,3,2:T(4,128)} dynamic-update-slice(f32[3,256,20,64]{1,0,3,2:T(4,128)} %get-tuple-element.1186, f32[1,256,20,64]{1,0,3,2:T(1,128)S(1)} %copy.167, s32[]{:T(128)S(6)} %copy.177, s32[]{:T(128)} %constant.175.clone.1..sunk.2, s32[]{:T(128)} %constant.175.clone.1..sunk.2, s32[]{:T(128)} %constant.175.clone.1..sunk.2) | dynamic-update-slice | bytes 2621444 | tf_op jit(solution)/shard_map/jvp()/while/body/jit(dynamic_update_index_in_dim)/dynamic_update_slice | solution.py:63
  127.0 7.5 %fusion.170 = f32[256,20,64]{0,2,1:T(8,128)S(1)} fusion(f32[256,256]{1,0:T(8,128)S(1)} %fusion.169, f32[20,256]{1,0:T(8,128)S(1)} %bitcast.291, pred[256,256]{1,0:T(8,128)(4,1)S(1)} %get-tuple-element.1208, f32[3,256,20,64]{1,3,2,0:T(8,128)} %get-tuple-element.1204, s32[]{:T(128)S(6)} %copy.177, f32[256,20]{0,1:T(8,128)S(1)} %fusion.167), kind=kOutput, calls=%fused_computation.22.clone.1 | convolution fusion | flops 1012203520 | bytes 3022852 | tf_op jit(solution)/shard_map/jvp()/while/body/eval_jaxpr/hts,shp->thp/dot_general | solution.py:44
  141.3 29.0 %dynamic_update_slice.47 = f32[3,256,20,64]{1,0,3,2:T(4,128)} dynamic-update-slice(f32[3,256,20,64]{1,0,3,2:T(4,128)} %get-tuple-element.1186, f32[1,256,20,64]{1,0,3,2:T(1,128)S(1)} %copy.167, s32[]{:T(128)S(6)} %copy.177, s32[]{:T(128)} %constant.175.clone.1..sunk.2, s32[]{:T(128)} %constant.175.clone.1..sunk.2, s32[]{:T(128)} %constant.175.clone.1..sunk.2) | dynamic-update-slice | bytes 2621444 | tf_op jit(solution)/shard_map/jvp()/while/body/jit(dynamic_update_index_in_dim)/dynamic_update_slice | solution.py:63
  173.6 23.8 %all-reduce.2 = f32[160]{0:T(256)S(1)} all-reduce(f32[160]{0:T(256)S(1)} %fusion.106), channel_id=2, replica_groups=mesh['seq'=8,'chan'=4] {'seq'}, use_global_device_ids=true, to_apply=%add.2 | all-reduce | flops 160 | bytes 1280
  199.6 7.5 %reshape.309 = f32[768,20,64]{0,2,1:T(8,128)} reshape(f32[3,256,20,64]{1,0,3,2:T(4,128)} %get-tuple-element.611) | data formatting | bytes 7864320 | tf_op jit(solution)/shard_map/jvp()/reshape | solution.py:64
  207.2 53.0 %all-gather.9.cloned.1.call-done = f32[160,64,128]{2,1,0:T(8,128)} async-done(((f32[20,64,128]{2,1,0:T(8,128)}), f32[160,64,128]{2,1,0:T(8,128)}) %all-gather.9.cloned.1.call-update) | async-done | bytes 5242896 | tf_op jit(solution)/shard_map/all_gather | solution.py:17
  260.2 10.4 %while.67 = (s32[]{:T(128)}, f32[20,64,128]{2,1,0:T(8,128)S(1)}, s32[]{:T(128)}, f32[8,20]{1,0:T(8,128)S(1)}, f32[8,20,64,128]{3,2,1,0:T(8,128)}, /*index=5*/s32[]{:T(128)}, s32[]{:T(128)}) while((s32[]{:T(128)}, f32[20,64,128]{2,1,0:T(8,128)S(1)}, s32[]{:T(128)}, f32[8,20]{1,0:T(8,128)S(1)}, f32[8,20,64,128]{3,2,1,0:T(8,128)}, ...), condition=%wide.region_8.9_spmd.clone, body=%wide.region_7.8_spmd.clone.sunk | while | flops 655364 | bytes 1966433 | solution.py:30
  283.2 79.2 %all-gather.7.cloned.1.call-done = bf16[2560,1280]{1,0:T(8,128)(2,1)} async-done(((bf16[320,1280]{1,0:T(8,128)(2,1)}), bf16[2560,1280]{1,0:T(8,128)(2,1)}) %all-gather.7.cloned.1.call-update) | async-done | bytes 6553616 | tf_op jit(solution)/shard_map/all_gather | solution.py:103
  362.5 11.1 %multiply_reduce_fusion.3 = (f32[768]{0:T(1024)S(1)}, f32[768]{0:T(1024)S(1)}, bf16[768,1280]{1,0:T(8,128)(2,1)}) fusion(f32[768,1280]{1,0:T(8,128)} %copy.101, bf16[768,1280]{1,0:T(8,128)(2,1)S(1)} %copy-done.6, f32[1280]{0:T(1024)S(1)} %copy-done.13, bf16[768,2560]{1,0:T(8,128)(2,1)} %param.27, bf16[2560,1280]{1,0:T(8,128)(2,1)} %all-gather.7.cloned.1.call-done), kind=kOutput, calls=%fused_computation.140 | convolution fusion | flops 5045942272 | bytes 18361344 | tf_op jit(solution)/shard_map/dot_general | solution.py:101
  396.4 11.3 %convolution_bitcast_fusion = f32[2560,1280]{0,1:T(8,128)} fusion(bf16[768,2560]{1,0:T(8,128)(2,1)} %param.27, f32[1280]{0:T(1024)S(1)} %copy-done.13, f32[768]{0:T(1024)S(1)} %get-tuple-element.907, f32[768,1280]{1,0:T(8,128)} %copy.101, bf16[768,1280]{1,0:T(8,128)(2,1)S(1)} %copy-done.6), kind=kOutput, calls=%fused_computation.120 | convolution fusion | flops 5042012160 | bytes 22945792 | tf_op jit(solution)/shard_map/dot_general | solution.py:121
  407.7 14.0 %copy.122 = f32[2560,1280]{1,0:T(8,128)} copy(f32[2560,1280]{0,1:T(8,128)} %convolution_bitcast_fusion) | data formatting | bytes 26214400
  421.7 7.7 %reshape.338 = f32[3,256,20,64]{3,2,1,0:T(8,128)} reshape(f32[768,1280]{1,0:T(8,128)} %get-tuple-element.904) | data formatting | bytes 7864320 | tf_op jit(solution)/shard_map/transpose(jvp())/reshape;reshape | solution.py:64
  441.9 7.8 %copy.106 = f32[3,256,20,64]{1,3,2,0:T(8,128)} copy(f32[3,256,20,64]{3,2,1,0:T(8,128)} %reshape.338) | data formatting | bytes 7864320 | tf_op jit(solution)/shard_map/transpose(jvp())/while | solution.py:63
  449.7 31.0 %all-gather.11.cloned.1.call-done = f32[160,64,128]{2,1,0:T(8,128)} async-done(((f32[20,64,128]{2,1,0:T(8,128)}), f32[160,64,128]{2,1,0:T(8,128)}) %all-gather.11.cloned.1.call-update) | async-done | bytes 5242896 | tf_op jit(solution)/shard_map/all_gather | solution.py:17
  480.6 10.4 %while.68 = (s32[]{:T(128)}, f32[20,64,128]{2,1,0:T(8,128)S(1)}, s32[]{:T(128)}, f32[8,20]{1,0:T(8,128)S(1)}, f32[8,20,64,128]{3,2,1,0:T(8,128)}, /*index=5*/s32[]{:T(128)}, s32[]{:T(128)}, s32[]{:T(128)}, s32[]{:T(128)}) while((s32[]{:T(128)}, f32[20,64,128]{2,1,0:T(8,128)S(1)}, s32[]{:T(128)}, f32[8,20]{1,0:T(8,128)S(1)}, ...), condition=%wide.region_14.15_spmd.clone, body=%wide.region_13.14_spmd.clone.sunk | while | flops 655368 | bytes 1966495 | solution.py:30
  494.1 130.7 %while.66 = (s32[]{:T(128)}, f32[20,64,128]{2,1,0:T(8,128)S(1)}, bf16[3,256,20,64]{1,3,2,0:T(8,128)(2,1)}, f32[3,20,256]{2,1,0:T(8,128)}, f32[3,20,64,128]{3,2,1...) while((s32[]{:T(128)}, f32[20,64,128]{2,1,0:T(8,128)S(1)}, ...), condition=%wide.region_26.27_spmd, body=%wide.region_15.26_spmd.sunk | while | flops 3646282752 | bytes 32237720 | solution.py:63
  512.8 8.4 %fusion.153 = (f32[20,256]{1,0:T(8,128)}, f32[20,256]{1,0:T(8,128)}) fusion(f32[256,256]{1,0:T(8,128)S(1)} %fusion.152, f32[20,256]{1,0:T(8,128)S(1)} %bitcast.282, pred[256,256]{1,0:T(8,128)(4,1)} %iota_compare_fusion.3, f32[256,20,64]{0,2,1:T(8,128)S(1)} %get-tuple-element.1132, f32[256,20]{0,1:T(8,128)} %bitcast.286, ...), kind=kOutput, calls=%fused_computation.65.clone.1 | convolution fusion | flops 1017436160 | bytes 3031040 | tf_op jit(solution)/shard_map/transpose(jvp())/while/body/eval_jaxpr/checkpoint/hts,shp->thp/dot_general | solution.py:44
  556.3 8.4 %fusion.153 = (f32[20,256]{1,0:T(8,128)}, f32[20,256]{1,0:T(8,128)}) fusion(f32[256,256]{1,0:T(8,128)S(1)} %fusion.152, f32[20,256]{1,0:T(8,128)S(1)} %bitcast.282, pred[256,256]{1,0:T(8,128)(4,1)} %iota_compare_fusion.3, f32[256,20,64]{0,2,1:T(8,128)S(1)} %get-tuple-element.1132, f32[256,20]{0,1:T(8,128)} %bitcast.286, ...), kind=kOutput, calls=%fused_computation.65.clone.1 | convolution fusion | flops 1017436160 | bytes 3031040 | tf_op jit(solution)/shard_map/transpose(jvp())/while/body/eval_jaxpr/checkpoint/hts,shp->thp/dot_general | solution.py:44
  599.8 8.4 %fusion.153 = (f32[20,256]{1,0:T(8,128)}, f32[20,256]{1,0:T(8,128)}) fusion(f32[256,256]{1,0:T(8,128)S(1)} %fusion.152, f32[20,256]{1,0:T(8,128)S(1)} %bitcast.282, pred[256,256]{1,0:T(8,128)(4,1)} %iota_compare_fusion.3, f32[256,20,64]{0,2,1:T(8,128)S(1)} %get-tuple-element.1132, f32[256,20]{0,1:T(8,128)} %bitcast.286, ...), kind=kOutput, calls=%fused_computation.65.clone.1 | convolution fusion | flops 1017436160 | bytes 3031040 | tf_op jit(solution)/shard_map/transpose(jvp())/while/body/eval_jaxpr/checkpoint/hts,shp->thp/dot_general | solution.py:44
  639.2 58.9 %reduce-scatter.4.cloned.1.call-done = f32[320,1280]{1,0:T(8,128)} async-done(((f32[2560,1280]{1,0:T(8,128)}), f32[320,1280]{1,0:T(8,128)}) %reduce-scatter.4.cloned.1.call-update) | async-done | bytes 1638416
  (360 shorter events, 247.9 us)
Async XLA Ops:
  7.2 253.0 %all-gather.9.cloned.1.call-start = ((), (), s32[]{:S(2)}) async-start(), calls=%async_computation.2 | async-start | bytes 5898240 | tf_op jit(solution)/shard_map/all_gather | solution.py:17
  7.9 165.4 %copy-start.14 = (f32[20]{0:T(128)}, f32[20]{0:T(128)S(1)}, u32[]{:S(2)}) copy-start(f32[20]{0:T(128)S(1)} %get-tuple-element.911) | copy-start | bytes 244
  20.1 7.8 %copy-start.12 = (f32[20]{0:T(128)S(1)}, f32[20]{0:T(128)}, u32[]{:S(2)}) copy-start(f32[20]{0:T(128)} %param.24) | copy-start | bytes 244
  27.9 144.1 %copy-start.20 = (u32[32]{0:T(128)S(1)}, u32[32]{0:T(128)}, u32[]{:S(2)}) copy-start(u32[32]{0:T(128)} %constant.188) | copy-start | bytes 388
  27.9 145.4 %copy-start.8 = (f32[20,768]{1,0:T(8,128)S(1)}, f32[20,768]{1,0:T(8,128)}, u32[]{:S(2)}) copy-start(f32[20,768]{1,0:T(8,128)} %param.22) | copy-start | bytes 184324
  27.9 145.6 %copy-start.17 = (f32[20]{0:T(128)S(1)}, f32[20]{0:T(128)}, u32[]{:S(2)}) copy-start(f32[20]{0:T(128)} %param.23) | copy-start | bytes 244
  171.2 191.3 %all-gather.7.cloned.1.call-start = ((), (), s32[]{:S(2)}) async-start(), calls=%async_computation.1 | async-start | bytes 7372800 | tf_op jit(solution)/shard_map/all_gather | solution.py:103
  171.9 308.7 %all-gather.11.cloned.1.call-start = ((), (), s32[]{:S(2)}) async-start(), calls=%async_computation.3 | async-start | bytes 5898240 | tf_op jit(solution)/shard_map/all_gather | solution.py:17
  260.2 10.4 %copy-start.7 = (bf16[768,128]{1,0:T(8,128)(2,1)S(1)}, bf16[768,128]{1,0:T(8,128)(2,1)}, u32[]{:S(2)}) copy-start(bf16[768,128]{1,0:T(8,128)(2,1)} %param.21) | copy-start | bytes 589828
  277.6 84.9 %copy-start.6 = (bf16[768,1280]{1,0:T(8,128)(2,1)S(1)}, bf16[768,1280]{1,0:T(8,128)(2,1)}, u32[]{:S(2)}) copy-start(bf16[768,1280]{1,0:T(8,128)(2,1)} %param.19) | copy-start | bytes 5898244
  277.6 84.9 %copy-start.13 = (f32[1280]{0:T(1024)S(1)}, f32[1280]{0:T(1024)}, u32[]{:S(2)}) copy-start(f32[1280]{0:T(1024)} %param.25) | copy-start | bytes 15364
  396.1 301.9 %reduce-scatter.4.cloned.1.call-start = ((), (), s32[]{:S(2)}) async-start(), calls=%async_computation.4 | async-start | bytes 14745600
  500.4 8.7 %copy-start.10 = (f32[20]{0:T(128)}, f32[20]{0:T(128)S(1)}, u32[]{:S(2)}) copy-start(f32[20]{0:T(128)S(1)} %neg.73) | copy-start | bytes 244 | tf_op jit(solution)/shard_map/transpose(jvp())/while
  510.9 12.6 %copy-start.2 = (f32[3,8,2,128]{3,1,2,0:T(8,128)}, f32[3,8,2,128]{3,1,2,0:T(8,128)S(1)}, u32[]{:S(2)}) copy-start(f32[3,8,2,128]{3,1,2,0:T(8,128)S(1)} %copy.158) | copy-start | bytes 73732 | tf_op jit(solution)/shard_map/transpose(jvp())/while
  512.8 8.4 %copy-start.3 = (f32[256,256]{1,0:T(8,128)}, f32[256,256]{1,0:T(8,128)S(1)}, u32[]{:S(2)}) copy-start(f32[256,256]{1,0:T(8,128)S(1)} %fusion.152) | copy-start | bytes 786436 | tf_op jit(solution)/shard_map/transpose(jvp())/while
  512.8 8.4 %copy-start.5 = (f32[20,256]{1,0:T(8,128)S(1)}, f32[20,256]{1,0:T(8,128)}, u32[]{:S(2)}) copy-start(f32[20,256]{1,0:T(8,128)} %dynamic-slice_bitcast_fusion.16) | copy-start | bytes 61444 | tf_op jit(solution)/shard_map/transpose(jvp())/while
  543.9 8.7 %copy-start.10 = (f32[20]{0:T(128)}, f32[20]{0:T(128)S(1)}, u32[]{:S(2)}) copy-start(f32[20]{0:T(128)S(1)} %neg.73) | copy-start | bytes 244 | tf_op jit(solution)/shard_map/transpose(jvp())/while
  554.4 12.6 %copy-start.2 = (f32[3,8,2,128]{3,1,2,0:T(8,128)}, f32[3,8,2,128]{3,1,2,0:T(8,128)S(1)}, u32[]{:S(2)}) copy-start(f32[3,8,2,128]{3,1,2,0:T(8,128)S(1)} %copy.158) | copy-start | bytes 73732 | tf_op jit(solution)/shard_map/transpose(jvp())/while
  556.3 8.4 %copy-start.3 = (f32[256,256]{1,0:T(8,128)}, f32[256,256]{1,0:T(8,128)S(1)}, u32[]{:S(2)}) copy-start(f32[256,256]{1,0:T(8,128)S(1)} %fusion.152) | copy-start | bytes 786436 | tf_op jit(solution)/shard_map/transpose(jvp())/while
  556.3 8.4 %copy-start.5 = (f32[20,256]{1,0:T(8,128)S(1)}, f32[20,256]{1,0:T(8,128)}, u32[]{:S(2)}) copy-start(f32[20,256]{1,0:T(8,128)} %dynamic-slice_bitcast_fusion.16) | copy-start | bytes 61444 | tf_op jit(solution)/shard_map/transpose(jvp())/while
  587.4 8.7 %copy-start.10 = (f32[20]{0:T(128)}, f32[20]{0:T(128)S(1)}, u32[]{:S(2)}) copy-start(f32[20]{0:T(128)S(1)} %neg.73) | copy-start | bytes 244 | tf_op jit(solution)/shard_map/transpose(jvp())/while
  597.9 12.6 %copy-start.2 = (f32[3,8,2,128]{3,1,2,0:T(8,128)}, f32[3,8,2,128]{3,1,2,0:T(8,128)S(1)}, u32[]{:S(2)}) copy-start(f32[3,8,2,128]{3,1,2,0:T(8,128)S(1)} %copy.158) | copy-start | bytes 73732 | tf_op jit(solution)/shard_map/transpose(jvp())/while
  599.8 8.4 %copy-start.3 = (f32[256,256]{1,0:T(8,128)}, f32[256,256]{1,0:T(8,128)S(1)}, u32[]{:S(2)}) copy-start(f32[256,256]{1,0:T(8,128)S(1)} %fusion.152) | copy-start | bytes 786436 | tf_op jit(solution)/shard_map/transpose(jvp())/while
  599.8 8.4 %copy-start.5 = (f32[20,256]{1,0:T(8,128)S(1)}, f32[20,256]{1,0:T(8,128)}, u32[]{:S(2)}) copy-start(f32[20,256]{1,0:T(8,128)} %dynamic-slice_bitcast_fusion.16) | copy-start | bytes 61444 | tf_op jit(solution)/shard_map/transpose(jvp())/while
  (19 other events, 107.3 us)
Sparse Core Ops, SparseCore 0:
  171.3 88.8 all-gather.8
  262.3 100.0 all-gather.6
  396.3 84.3 all-gather.10
  484.7 213.2 reduce-scatter.3
where the time goes:
time: 719 us; the launch traced here: 705 us
  waiting for transfers between devices  223 us (31%)
  local copies, waits for them, and re-layouts  213 us (30%)
  matrix products  140 us (19%)
  other arithmetic  82.7 us (12%)
  blocking collectives  29.6 us (4%)
  between operations  15.1 us (2%)
    dynamic_update_slice x6, local copies, waits for them, and re-layouts, ssd_local(): lax.scan(stepper, state_in, (x_blocks, dt_blocks, b_blocks, c_blocks))  91 us
    all_gather x2, waiting for transfers between devices, entering(): everything = jax.tree.map(lambda part: lax.all_gather(part, axis), value)  84 us
    all_gather x1, waiting for transfers between devices, shards(): lax.all_gather(out_weight, 'seq', axis=0, tiled=True)  79.2 us
    dot_general x9, matrix products, group_step(): jnp.einsum('hts,shp->thp', decay_mat * affinity[None], weighted, precisio...  68.2 us
    unnamed x5, waiting for transfers between devices  59.6 us
    unnamed x37, local copies, waits for them, and re-layouts  37.3 us
    another operation x33, other arithmetic  27.5 us
    unnamed x1, blocking collectives  23.8 us
  transfers between devices with their start and end apart: 4, of which 4 were waited for; matrix products, arithmetic and copies ran while one was open for 34% of the time, Pallas kernels for 0%

commit v1 on v0

v1 whole, which is shorter than its diff:
```python
from functools import partial

import jax
import jax.numpy as jnp
from jax import lax
from jax.experimental import pallas as pl
from jax.experimental.pallas import tpu as pltpu
from jax.sharding import PartitionSpec as P

CHUNK = 128
LANES = 128
norm_eps = 1e-05
highest = lax.Precision.HIGHEST
f32 = jnp.float32
bf16 = jnp.bfloat16


def mm(a, b, dims=((1,), (0,))):
    return lax.dot_general(a.astype(bf16), b.astype(bf16), (dims, ((), ())), preferred_element_type=f32)


def split(v):
    hi = v.astype(bf16)
    return hi, (v - hi.astype(f32)).astype(bf16)


def head_of(width, size):
    rows = lax.broadcasted_iota(jnp.int32, (LANES, width), 0)
    cols = lax.broadcasted_iota(jnp.int32, (LANES, width), 1)
    return jnp.where((cols >= rows * size) & (cols < (rows + 1) * size), 1.0, 0.0).astype(bf16)


def expand(v, select):
    hi, lo = split(v)
    return mm(jnp.concatenate([hi, lo], axis=1), jnp.concatenate([select, select], axis=0))


def per_head(v, select):
    hi, lo = split(v)
    return mm(hi, select, ((1,), (1,))) + mm(lo, select, ((1,), (1,)))


def run_sum(log_step):
    rows = lax.broadcasted_iota(jnp.int32, (CHUNK, CHUNK), 0)
    cols = lax.broadcasted_iota(jnp.int32, (CHUNK, CHUNK), 1)
    upper = jnp.where(rows <= cols, 1.0, 0.0)
    return jnp.dot(log_step, upper, precision=highest, preferred_element_type=f32)


def state_kernel(size, x_ref, b_ref, step_ref, dt_ref, out_ref):
    @pl.when(pl.program_id(0) == 0)
    def _():
        out_ref[...] = jnp.zeros_like(out_ref)

    select = head_of(x_ref.shape[1], size)
    log_row = run_sum(step_ref[...])
    last = log_row[:, CHUNK - 1 :]
    weight = jnp.transpose(jnp.exp(last - log_row) * dt_ref[...])
    whole = jnp.transpose(jnp.broadcast_to(jnp.exp(last), (LANES, CHUNK)))
    scaled = expand(weight, select) * x_ref[...].astype(f32)
    out_ref[...] = expand(whole[:8], select)[:1] * out_ref[...] + mm(b_ref[...], scaled, ((0,), (0,)))


def pair_decay(log_row, log_col, head):
    rows = lax.broadcasted_iota(jnp.int32, (CHUNK, CHUNK), 0)
    cols = lax.broadcasted_iota(jnp.int32, (CHUNK, CHUNK), 1)
    causal = rows >= cols
    parts = []
    for h in (head, head + 1):
        gap = log_col[:, h : h + 1] - log_row[h : h + 1, :]
        parts.append(jnp.where(causal, jnp.exp(jnp.where(causal, gap, 0.0)), 0.0))
    return parts


def forward_kernel(
    size, x_ref, z_ref, g_ref, b_ref, c_ref, step_ref, dt_ref, skip_ref, gain_ref, first_ref,
    y_ref, stat_ref, saved_ref, state_ref
):
    @pl.when(pl.program_id(0) == 0)
    def _():
        state_ref[...] = first_ref[...]

    width = x_ref.shape[1]
    select = head_of(width, size)
    log_row = run_sum(step_ref[...])
    log_col = jnp.transpose(log_row)
    last = log_row[:, CHUNK - 1 :]
    dt_row = dt_ref[...]
    weight = jnp.transpose(jnp.exp(last - log_row) * dt_row)
    whole = jnp.transpose(jnp.broadcast_to(jnp.exp(last), (LANES, CHUNK)))
    x_vals = x_ref[...]
    x_wide = x_vals.astype(f32)
    state = state_ref[...]
    saved_ref[0] = state.astype(bf16)
    affinity = mm(c_ref[...], b_ref[...], ((1,), (1,)))
    base = expand(jnp.exp(log_col), select) * mm(c_ref[...], state) + skip_ref[...] * x_wide
    lane = lax.broadcasted_iota(jnp.int32, (CHUNK, 2 * size), 1)
    squares = jnp.zeros((CHUNK, 2 * size), f32)
    dots = jnp.zeros((CHUNK, 2 * size), f32)
    for pair in range(width // (2 * size)):
        at = slice(pair * 2 * size, (pair + 1) * 2 * size)
        mats = pair_decay(log_row, log_col, 2 * pair)
        mats = [
            (m * affinity * dt_row[2 * pair + i : 2 * pair + i + 1, :]).astype(bf16)
            for i, m in enumerate(mats)
        ]
        xp = x_vals[:, at]
        zero = jnp.zeros_like(xp)
        stacked = jnp.concatenate([jnp.where(lane < size, xp, zero), jnp.where(lane < size, zero, xp)], axis=0)
        y_pair = base[:, at] + mm(jnp.concatenate(mats, axis=1), stacked)
        y_ref[:, at] = y_pair
        z_pair = z_ref[:, at].astype(f32)
        gated = y_pair * z_pair / (1.0 + jnp.exp(-z_pair))
        squares += gated * gated
        dots += gated * g_ref[:, at].astype(f32) * gain_ref[:, at]
    stat_ref[:, 0:1] = jnp.sum(squares, axis=1, keepdims=True)
    stat_ref[:, 1:2] = jnp.sum(dots, axis=1, keepdims=True)
    scaled = expand(weight, select) * x_wide
    state_ref[...] = expand(whole[:8], select)[:1] * state + mm(b_ref[...], scaled, ((0,), (0,)))


def gate_kernel(
    size, y_ref, z_ref, g_ref, c_ref, step_ref, gain_ref, scale_ref, normed_ref, dy_ref, dz_ref, out_ref
):
    @pl.when(pl.program_id(0) == 0)
    def _():
        out_ref[...] = jnp.zeros_like(out_ref)

    select = head_of(y_ref.shape[1], size)
    inverse = scale_ref[:, 0:1]
    pull = scale_ref[:, 1:2]
    y_vals = y_ref[...]
    z_vals = z_ref[...].astype(f32)
    sig = 1.0 / (1.0 + jnp.exp(-z_vals))
    act = z_vals * sig
    gated = y_vals * act
    gain = gain_ref[...]
    normed_ref[...] = (gated * inverse * gain).astype(bf16)
    grad = inverse * (g_ref[...].astype(f32) * gain) - gated * pull
    dz_ref[...] = (grad * y_vals * sig * (1.0 + z_vals * (1.0 - sig))).astype(bf16)
    dy = grad * act
    dy_ref[...] = dy.astype(bf16)
    log_row = run_sum(step_ref[...])
    growth = jnp.transpose(jnp.exp(log_row))
    out_ref[...] = expand(growth[CHUNK - 8 :], select)[7:8] * out_ref[...] + mm(
        c_ref[...], expand(growth, select) * dy, ((0,), (0,))
    )


def backward_kernel(
    size, x_ref, dy_ref, b_ref, c_ref, step_ref, dt_ref, rate_ref, skip_ref, saved_ref, end_ref,
    dx_ref, ddt_ref, grad_ref, row_ref, col_ref
):
    @pl.when(pl.program_id(0) == 0)
    def _():
        grad_ref[...] = end_ref[...]
        row_ref[...] = jnp.zeros_like(row_ref)
        col_ref[...] = jnp.zeros_like(col_ref)

    width = x_ref.shape[1]
    select = head_of(width, size)
    log_row = run_sum(step_ref[...])
    log_col = jnp.transpose(log_row)
    last = log_row[:, CHUNK - 1 :]
    dt_row = dt_ref[...]
    to_end = jnp.exp(last - log_row)
    grad = grad_ref[...]
    saved = saved_ref[0]
    x_vals = x_ref[...]
    x_wide = x_vals.astype(f32)
    dy_vals = dy_ref[...]
    dy_wide = dy_vals.astype(f32)
    affinity = mm(c_ref[...], b_ref[...], ((1,), (1,)))
    from_end = mm(b_ref[...], grad)
    growth = jnp.exp(log_col)
    grown = expand(growth, select) * dy_wide
    carried = jnp.transpose(per_head(grown * mm(c_ref[...], saved), select))
    inner = jnp.transpose(per_head(x_wide * from_end, select)) * to_end
    product = jnp.sum(saved.astype(f32) * grad, axis=0, keepdims=True)
    product = jnp.transpose(per_head(jnp.broadcast_to(product, (LANES, width)), select))[:, :1]
    dxw = expand(jnp.transpose(to_end), select) * from_end
    dt_wide = expand(jnp.transpose(dt_row), select)
    skip_dy = skip_ref[...] * dy_wide
    lane = lax.broadcasted_iota(jnp.int32, (CHUNK, 2 * size), 1)
    for pair in range(width // (2 * size)):
        at = slice(pair * 2 * size, (pair + 1) * 2 * size)
        mats = [m * affinity for m in pair_decay(log_row, log_col, 2 * pair)]
        xp = x_vals[:, at]
        dyp = dy_vals[:, at]
        zero = jnp.zeros_like(xp)
        stacked = jnp.concatenate([jnp.where(lane < size, xp, zero), jnp.where(lane < size, zero, xp)], axis=0)
        prods = mm(dyp, stacked, ((1,), (1,)))
        for i in range(2):
            h = 2 * pair + i
            both = mats[i] * prods[:, i * CHUNK : (i + 1) * CHUNK]
            row_ref[h : h + 1, :] = jnp.sum(both, axis=0, keepdims=True)
            col_ref[:, h : h + 1] = jnp.sum(both * dt_row[h : h + 1, :], axis=1, keepdims=True)
        inside = mm(jnp.concatenate([m.astype(bf16) for m in mats], axis=1), dyp, ((0,), (0,)))
        inside = jnp.where(lane < size, inside[:CHUNK], inside[CHUNK:])
        dx_ref[:, at] = (dt_wide[:, at] * (dxw[:, at] + inside) + skip_dy[:, at]).astype(bf16)
    direct = row_ref[...]
    update = dt_row * inner
    d_log = jnp.transpose(col_ref[...]) - dt_row * direct + carried - update
    at_end = jnp.sum(update, axis=1, keepdims=True) + jnp.exp(last) * product
    rows = lax.broadcasted_iota(jnp.int32, (CHUNK, CHUNK), 0)
    cols = lax.broadcasted_iota(jnp.int32, (CHUNK, CHUNK), 1)
    lower = jnp.where(rows >= cols, 1.0, 0.0)
    later = jnp.dot(d_log, lower, precision=highest, preferred_element_type=f32) + at_end
    ddt_ref[...] = direct + inner - rate_ref[...] * later
    grad_ref[...] = expand(growth[CHUNK - 8 :], select)[7:8] * grad + mm(c_ref[...], grown, ((0,), (0,)))


def shards(
    x_in, z_gate, b_proj, c_proj, dt_step, a_log, skip_gain, norm_gain, out_weight, out_grad
):
    length, width = x_in.shape
    heads = a_log.shape[0]
    size = width // heads
    states = b_proj.shape[1]
    blocks = length // CHUNK
    peers, index = lax.axis_size("seq"), lax.axis_index("seq")

    def tok(w, rev=False):
        return pl.BlockSpec((CHUNK, w), lambda i: (blocks - 1 - i, 0) if rev else (i, 0))

    def row(rev=False):
        return pl.BlockSpec((LANES, CHUNK), lambda i: (0, blocks - 1 - i) if rev else (0, i))

    def all_of(r, w):
        return pl.BlockSpec((r, w), lambda i: (0, 0))

    def saved_at(rev=False):
        return pl.BlockSpec((1, states, width), lambda i: (blocks - 1 - i, 0, 0) if rev else (i, 0, 0))

    def shape(s, d):
        return jax.ShapeDtypeStruct(s, d)

    def call(kernel, name, ins, outs, out_shape, scratch=(), flops=10**9, moved=8 * 10**6):
        return pl.pallas_call(
            partial(kernel, size),
            grid=(blocks,),
            in_specs=ins,
            out_specs=outs,
            out_shape=out_shape,
            scratch_shapes=scratch,
            name=name,
            compiler_params=pltpu.CompilerParams(
                dimension_semantics=("arbitrary",), vmem_limit_bytes=48 * 1024 * 1024
            ),
            cost_estimate=pl.CostEstimate(flops=flops, bytes_accessed=moved, transcendentals=0),
        )

    weight_all = lax.all_gather(out_weight, "seq", axis=0, tiled=True)
    rates = jnp.exp(a_log)
    pad = ((0, LANES - heads), (0, 0))
    total = jnp.sum(-rates[:, None] * dt_step, axis=1)
    totals = lax.all_gather(total, "seq")
    dt_rows = jnp.pad(dt_step, pad)
    steps = jnp.pad(-rates[:, None] * dt_step, pad)
    rate_col = jnp.pad(rates[:, None], pad)
    skip = jnp.repeat(skip_gain, size)[None, :]
    gain = norm_gain[None, :]
    state_shape = shape((states, width), f32)
    full = all_of(states, width)

    local_state = call(
        state_kernel, "local_state", [tok(width), tok(states), row(), row()], full, state_shape
    )(x_in, b_proj, steps, dt_rows)
    weight_all, local_state = lax.optimization_barrier((weight_all, local_state))
    order = jnp.arange(peers)

    def entering(local, reverse):
        everything = lax.all_gather(local.astype(bf16), "seq")
        between = order[:, None] < order[None, :] if not reverse else order[:, None] > order[None, :]
        past = order < index if not reverse else order > index
        inside = (between & past[None, :]).astype(f32)
        decay = jnp.exp(jnp.sum(inside[:, :, None] * totals[None], axis=1))
        coef = jnp.where(past[:, None], decay, 0.0)
        coef = jnp.repeat(coef, size, axis=1)[:, None, :]
        return jnp.sum(coef * everything.astype(f32), axis=0)

    state_in = entering(local_state, False)
    grad_norm = jnp.dot(out_grad, weight_all, preferred_element_type=f32).astype(bf16)
    y_vals, stats, saved = call(
        forward_kernel,
        "scan_forward",
        [tok(width), tok(width), tok(width), tok(states), tok(states), row(), row(),
         all_of(1, width), all_of(1, width), full],
        (tok(width), tok(2), saved_at()),
        (shape((length, width), f32), shape((length, 2), f32), shape((blocks, states, width), bf16)),
        [pltpu.VMEM((states, width), f32)],
    )(x_in, z_gate, grad_norm, b_proj, c_proj, steps, dt_rows, skip, gain, state_in)
    sums = lax.psum(jnp.transpose(stats), "chan")
    full_width = width * lax.axis_size("chan")
    inverse = lax.rsqrt(sums[0] / full_width + norm_eps)
    scales = jnp.stack([inverse, inverse**3 * sums[1] / full_width], axis=1)
    normed, grad_y, grad_z, local_grad = call(
        gate_kernel,
        "gate_backward",
        [tok(width, True), tok(width, True), tok(width, True), tok(states, True), row(True),
         all_of(1, width), tok(2, True)],
        (tok(width, True), tok(width, True), tok(width, True), full),
        (shape((length, width), bf16),) * 3 + (state_shape,),
    )(y_vals, z_gate, grad_norm, c_proj, steps, gain, scales)
    grad_end = entering(local_grad, True)
    partial_weight = lax.dot_general(
        out_grad, normed, (((0,), (0,)), ((), ())), preferred_element_type=f32
    )
    weight_grad = reduce_rows(partial_weight, peers)
    grad_x, grad_dt = call(
        backward_kernel,
        "scan_backward",
        [tok(width, True), tok(width, True), tok(states, True), tok(states, True), row(True), row(True),
         all_of(LANES, 1), all_of(1, width), saved_at(True), full],
        (tok(width, True), row(True)),
        (shape((length, width), bf16), shape((LANES, length), f32)),
        [pltpu.VMEM((states, width), f32), pltpu.VMEM((LANES, CHUNK), f32), pltpu.VMEM((CHUNK, LANES), f32)],
    )(x_in, grad_y, b_proj, c_proj, steps, dt_rows, rate_col, skip, saved, grad_end)
    return (grad_x, grad_z, grad_dt[:heads], weight_grad)


def reduce_rows(value, peers):
    rows, width = value.shape
    parts = value.astype(bf16).reshape(peers, rows // peers, width)
    parts = lax.all_to_all(parts, "seq", 0, 0)
    return jnp.sum(parts.astype(f32), axis=0)


def solution(mesh):
    placed = (
        P("seq", "chan"),
        P("seq", "chan"),
        P("seq", None),
        P("seq", None),
        P("chan", "seq"),
        P("chan"),
        P("chan"),
        P("chan"),
        P("seq", "chan"),
        P("seq", None),
    )
    return jax.shard_map(
        shards,
        mesh=mesh,
        in_specs=placed,
        out_specs=(P("seq", "chan"), P("seq", "chan"), P("chan", "seq"), P("seq", "chan")),
        check_vma=False,
    )
```

time: 719 us -> 426 us (0.59); the launches traced: 705 us -> 425 us
  local copies, waits for them, and re-layouts: 213 us -> 19.8 us
  matrix products: 140 us -> 17.2 us
  other arithmetic: 82.7 us -> 17.6 us
  waiting for transfers between devices: 223 us -> 272 us
  Pallas kernels: 0 us -> 44.6 us
    dot_general x34 -> x2, matrix products: 140 us -> 17.2 us  [the longest x1 9.87 us: shards(): jnp.dot(out_grad, weight_all, preferred_element_type=f32).astype(bf16)]
    all_gather x3, waiting for transfers between devices: 163 us -> 269 us  [the longest x2 173 us: entering(): everything = lax.all_gather(local.astype(bf16), 'seq')]
    dynamic_update_slice x6 -> x0, local copies, waits for them, and re-layouts: 91 us -> none  [ssd_local(): lax.scan(stepper, state_in, (x_blocks, dt_blocks, b_blocks, c_blocks))]
    unnamed x5 -> x3, waiting for transfers between devices: 59.6 us -> 0.71 us
    pallas_call x0 -> x4, Pallas kernels: none -> 44.6 us  [the longest x1 17.7 us: shards(): call(backward_kernel, 'scan_backward', [tok(width, True), tok(width, True...]
    unnamed x37 -> x35, local copies, waits for them, and re-layouts: 37.3 us -> 7.23 us
    another operation x50 -> x2, local copies, waits for them, and re-layouts: 28.4 us -> 0.95 us  [the longest x1 0.87 us: shards(): scales = jnp.stack([inverse, inverse ** 3 * sums[1] / full_width], axis=1)]
    another operation x33 -> x1, other arithmetic: 27.5 us -> 0.6 us  [shards(): scales = jnp.stack([inverse, inverse ** 3 * sums[1] / full_width], axis=1)]
  transfers between devices with their start and end apart: 4 -> 4, of which waited for: 4 -> 4; matrix products, arithmetic and copies ran while one was open for 34% -> 5% of each run, Pallas kernels for 0% -> 5%
where the time goes in v1:
time: 426 us; the launch traced here: 425 us
  waiting for transfers between devices  272 us (64%)
  Pallas kernels  44.6 us (10%)
  blocking collectives  33.7 us (8%)
  local copies, waits for them, and re-layouts  19.8 us (5%)
  other arithmetic  17.6 us (4%)
  matrix products  17.2 us (4%)
  between operations  14.7 us (3%)
  starting transfers between devices  5.09 us (1%)
    all_gather x2, waiting for transfers between devices, entering(): everything = lax.all_gather(local.astype(bf16), 'seq')  173 us
    all_gather x1, waiting for transfers between devices, shards(): weight_all = lax.all_gather(out_weight, 'seq', axis=0, tiled=True)  95.8 us
    unnamed x1, blocking collectives  18.9 us
    pallas_call x1, Pallas kernels, shards(): call(backward_kernel, 'scan_backward', [tok(width, True), tok(width, True...  17.7 us
    psum x1, blocking collectives, shards(): sums = lax.psum(jnp.transpose(stats), 'chan')  14.8 us
    pallas_call x1, Pallas kernels, shards(): call(forward_kernel, 'scan_forward', [tok(width), tok(width), tok(width),...  12.2 us
    dot_general x1, matrix products, shards(): jnp.dot(out_grad, weight_all, preferred_element_type=f32).astype(bf16)  9.87 us
    convert_element_type x1, local copies, waits for them, and re-layouts, reduce_rows(): parts = value.astype(bf16).reshape(peers, rows // peers, width)  9.47 us
  transfers between devices with their start and end apart: 4, of which 4 were waited for; matrix products, arithmetic and copies ran while one was open for 5% of the time, Pallas kernels for 5%

profile of v1, /device:TPU:0, one launch (start us, length us, event | category | flops | bytes accessed | tf_op | source)
XLA Modules:
  0.0 424.8 jit_solution(7668991122194542867)
XLA Ops:
  8.9 1.3 exponential_bitcast_fusion
  10.2 1.1 fusion.13
  11.3 1.5 copy-done
  13.7 5.3 %local_state.1 = f32[128,1280]{1,0:T(8,128)S(1)} custom-call(bf16[768,1280]{1,0:T(8,128)(2,1)S(1)} %copy-done, bf16[768,128]{1,0:T(8,128)(2,1)S(1)} %copy-done.5, f32[128,768]{1,0:T(8,128)S(1)} %pad.11.step_ref, f32[128,768]{1,0:T(8,128)S(1)} %pad.12.dt_ref), custom_call_target="tpu_custom_call" | custom-call | flops 1000000000 | bytes 8000000 | tf_op jit(solution)/shard_map/local_state/pallas_call | solution.py:266
  19.1 95.8 %all-gather.7.cloned.1.call-done = bf16[2560,1280]{1,0:T(8,128)(2,1)} async-done(((bf16[320,1280]{1,0:T(8,128)(2,1)}), bf16[2560,1280]{1,0:T(8,128)(2,1)}) %all-gather.7.cloned.1.call-update) | async-done | bytes 6553616 | tf_op jit(solution)/shard_map/all_gather | solution.py:253
  117.3 18.9 %all-reduce.3 = f32[160]{0:T(256)S(1)} all-reduce(f32[160]{0:T(256)S(1)} %dynamic-update-slice), channel_id=2, replica_groups=mesh['seq'=8,'chan'=4] {'seq'}, use_global_device_ids=true, to_apply=%add.3 | all-reduce | flops 160 | bytes 1280
  137.8 9.9 %fusion.3.g_ref = bf16[768,1280]{1,0:T(8,128)(2,1)} fusion(bf16[768,2560]{1,0:T(8,128)(2,1)} %param.19, bf16[2560,1280]{1,0:T(8,128)(2,1)} %all-gather.7.cloned.1.call-done), kind=kOutput, calls=%fused_computation.8 | convolution fusion | flops 5034147840 | bytes 12451840 | tf_op jit(solution)/shard_map/dot_general | solution.py:283
  147.6 22.9 %all-gather.9.cloned.1.call-done = bf16[1024,1280]{1,0:T(8,128)(2,1)} async-done(((bf16[128,1280]{1,0:T(8,128)(2,1)}), bf16[1024,1280]{1,0:T(8,128)(2,1)}) %all-gather.9.cloned.1.call-update) | async-done | bytes 2621456 | tf_op jit(solution)/shard_map/all_gather | solution.py:273
  170.5 2.3 fusion.2.first_ref
  172.9 12.2 %scan_forward.1 = (f32[768,1280]{1,0:T(8,128)}, f32[768,2]{1,0:T(8,128)S(1)}, bf16[6,128,1280]{2,1,0:T(8,128)(2,1)S(1)}) custom-call(bf16[768,1280]{1,0:T(8,128)(2,1)S(1)} %copy-done.1, bf16[768,1280]{1,0:T(8,128)(2,1)} %z_ref.3, bf16[768,1280]{1,0:T(8,128)(2,1)} %fusion.3.g_ref, bf16[768,128]{1,0:T(8,128)(2,1)S(1)} %copy-done.6, ...), custom_call_target="tpu_custom_call" | custom-call | flops 1000000000 | bytes 8000000 | tf_op jit(solution)/shard_map/scan_forward/pallas_call | solution.py:284
  185.1 1.3 copy-done.2
  186.4 14.8 %psum.7 = f32[2,768]{0,1:T(8,128)} all-reduce(f32[2,768]{0,1:T(8,128)S(1)} %bitcast.17), channel_id=1, replica_groups=mesh['seq'=8,'chan'=4] {'chan'}, use_global_device_ids=true, to_apply=%region_3.4 | all-reduce | flops 1536 | bytes 12288 | tf_op jit(solution)/shard_map/psum | solution.py:293
  201.2 1.5 fusion.6
  204.2 9.4 %gate_backward.1 = (bf16[768,1280]{1,0:T(8,128)(2,1)S(1)}, bf16[768,1280]{1,0:T(8,128)(2,1)S(1)}, bf16[768,1280]{1,0:T(8,128)(2,1)}, f32[128,1280]{1,0:T(8,128)S(1)}) custom-call(f32[768,1280]{1,0:T(8,128)} %get-tuple-element.17.y_ref, bf16[768,1280]{1,0:T(8,128)(2,1)} %z_ref.3, bf16[768,1280]{1,0:T(8,128)(2,1)} %fusion.3.g_ref, ...), custom_call_target="tpu_custom_call" | custom-call | flops 1000000000 | bytes 8000000 | tf_op jit(solution)/shard_map/gate_backward/pallas_call | solution.py:297
  213.6 1.3 copy-done.3
  215.8 7.3 %fusion = bf16[2560,1280]{0,1:T(8,128)(2,1)} fusion(bf16[768,1280]{1,0:T(8,128)(2,1)S(1)} %get-tuple-element.25, bf16[768,2560]{1,0:T(8,128)(2,1)S(1)} %copy-done.14), kind=kOutput, calls=%fused_computation.2 | convolution fusion | flops 5036441600 | bytes 12451840 | tf_op jit(solution)/shard_map/dot_general | solution.py:306
  223.0 9.5 %copy.30 = bf16[2560,1280]{1,0:T(8,128)(2,1)} copy(bf16[2560,1280]{0,1:T(8,128)(2,1)} %fusion) | data formatting | bytes 13107200 | tf_op jit(solution)/shard_map/convert_element_type | solution.py:324
  232.5 4.8 %all-to-all-start = ((bf16[8,320,1280]{2,1,0:T(8,128)(2,1)}), bf16[8,320,1280]{2,1,0:T(8,128)(2,1)}, u32[]{:S(2)}, u32[]{:S(2)}) async-start(bf16[8,320,1280]{2,1,0:T(8,128)(2,1)} %bitcast.18), calls=%async_computation | async-start | bytes 13107200 | tf_op jit(solution)/shard_map/all_to_all | solution.py:325
  237.6 1.8 convert_element_type.51
  239.8 150.2 %all-gather.11.cloned.1.call-done = bf16[1024,1280]{1,0:T(8,128)(2,1)} async-done(((bf16[128,1280]{1,0:T(8,128)(2,1)}), bf16[1024,1280]{1,0:T(8,128)(2,1)}) %all-gather.11.cloned.1.call-update) | async-done | bytes 2621456 | tf_op jit(solution)/shard_map/all_gather | solution.py:273
  390.0 2.3 fusion.1.end_ref
  392.4 17.7 %scan_backward.1 = (bf16[768,1280]{1,0:T(8,128)(2,1)}, f32[128,768]{1,0:T(8,128)S(1)}) custom-call(bf16[768,1280]{1,0:T(8,128)(2,1)S(1)} %copy-done.1, bf16[768,1280]{1,0:T(8,128)(2,1)} %copy-done.3, bf16[768,128]{1,0:T(8,128)(2,1)S(1)} %copy-done.6, bf16[768,128]{1,0:T(8,128)(2,1)S(1)} %copy-done.4, f32[128,768]{1,0:T(8,128)S(1)} %pad.11.step_ref, ...), custom_call_target="tpu_custom_call" | custom-call | flops 1000000000 | bytes 8000000 | tf_op jit(solution)/shard_map/scan_backward/pallas_call | solution.py:310
  410.7 2.5 all-to-all-done
  413.2 5.1 %convert_reduce_fusion = f32[320,1280]{1,0:T(8,128)} fusion(bf16[8,320,1280]{2,1,0:T(8,128)(2,1)} %all-to-all-done), kind=kLoop, calls=%fused_computation | loop fusion | flops 6144000 | bytes 8192000 | tf_op jit(solution)/shard_map/reduce_sum | solution.py:326
  (62 shorter events, 9.5 us)
Async XLA Ops:
  7.2 108.6 %copy-start.15 = (u32[32]{0:T(128)S(1)}, u32[32]{0:T(128)}, u32[]{:S(2)}) copy-start(u32[32]{0:T(128)} %constant.24) | copy-start | bytes 388
  7.2 108.4 %copy-start.9 = (f32[1280]{0:T(1024)S(1)}, f32[1280]{0:T(1024)}, u32[]{:S(2)}) copy-start(f32[1280]{0:T(1024)} %param.17) | copy-start | bytes 15364
  7.2 108.5 %copy-start.12 = (f32[20]{0:T(128)S(1)}, f32[20]{0:T(128)}, u32[]{:S(2)}) copy-start(f32[20]{0:T(128)} %param.16) | copy-start | bytes 244
  7.2 107.6 %all-gather.7.cloned.1.call-start = ((), (), s32[]{:S(2)}) async-start(), calls=%async_computation.1 | async-start | bytes 7372800 | tf_op jit(solution)/shard_map/all_gather | solution.py:253
  7.9 162.6 %all-gather.9.cloned.1.call-start = ((), (), s32[]{:S(2)}) async-start(), calls=%async_computation.2 | async-start | bytes 2949120 | tf_op jit(solution)/shard_map/all_gather | solution.py:273
  11.3 1.5 copy-start
  12.8 0.9 copy-start.5
  136.3 0.5 copy-start.10
  137.7 35.1 %copy-start.4 = (bf16[768,128]{1,0:T(8,128)(2,1)S(1)}, bf16[768,128]{1,0:T(8,128)(2,1)}, u32[]{:S(2)}) copy-start(bf16[768,128]{1,0:T(8,128)(2,1)} %c_ref.5) | copy-start | bytes 589828
  137.8 35.1 %copy-start.6 = (bf16[768,128]{1,0:T(8,128)(2,1)S(1)}, bf16[768,128]{1,0:T(8,128)(2,1)}, u32[]{:S(2)}) copy-start(bf16[768,128]{1,0:T(8,128)(2,1)} %b_ref.5) | copy-start | bytes 589828
  147.6 25.3 %copy-start.1 = (bf16[768,1280]{1,0:T(8,128)(2,1)S(1)}, bf16[768,1280]{1,0:T(8,128)(2,1)}, u32[]{:S(2)}) copy-start(bf16[768,1280]{1,0:T(8,128)(2,1)} %x_ref.5) | copy-start | bytes 5898244
  185.1 1.3 copy-start.2
  204.2 11.5 %copy-start.14 = (bf16[768,2560]{1,0:T(8,128)(2,1)S(1)}, bf16[768,2560]{1,0:T(8,128)(2,1)}, u32[]{:S(2)}) copy-start(bf16[768,2560]{1,0:T(8,128)(2,1)} %param.19) | copy-start | bytes 11796484
  213.6 1.3 copy-start.3
  214.9 0.8 copy-start.7
  232.5 6.9 %copy-start.13 = (f32[20,1]{0,1:T(1,128)S(1)}, f32[20,1]{0,1:T(1,128)}, u32[]{:S(2)}) copy-start(f32[20,1]{0,1:T(1,128)} %get-tuple-element.32) | copy-start | bytes 244
  232.5 7.0 %copy-start.8 = (f32[8,20]{1,0:T(8,128)S(1)}, f32[8,20]{1,0:T(8,128)}, u32[]{:S(2)}) copy-start(f32[8,20]{1,0:T(8,128)} %get-tuple-element.28) | copy-start | bytes 1924
  232.5 7.0 %copy-start.11 = (pred[8]{0:T(512)(128)(4,1)S(1)}, pred[8]{0:T(512)(128)(4,1)}, u32[]{:S(2)}) copy-start(pred[8]{0:T(512)(128)(4,1)} %copy-done.10) | copy-start | bytes 28
  232.5 180.7 %all-to-all-start = ((bf16[8,320,1280]{2,1,0:T(8,128)(2,1)}), bf16[8,320,1280]{2,1,0:T(8,128)(2,1)}, u32[]{:S(2)}, u32[]{:S(2)}) async-start(bf16[8,320,1280]{2,1,0:T(8,128)(2,1)} %bitcast.18), calls=%async_computation | async-start | bytes 13107200 | tf_op jit(solution)/shard_map/all_to_all | solution.py:325
  237.3 152.7 %all-gather.11.cloned.1.call-start = ((), (), s32[]{:S(2)}) async-start(), calls=%async_computation.3 | async-start | bytes 2949120 | tf_op jit(solution)/shard_map/all_gather | solution.py:273
Sparse Core Ops, SparseCore 0:
  10.2 104.5 all-gather.6
  117.6 52.9 all-gather.8
  240.9 149.0 all-gather.10
